TPU v7x, 32 devices: a whole 2x2x4 slice. The times are simulated.
32 devices in a mesh: strip: 4 (over z), tile: 8 (over y, x, core).
Axes of the slice: x: 2, y: 2, z: 4, core: 2. Of those that a mesh axis runs over, the one named last changes fastest.
Arguments:
- coords: float32 [1536, 3, 128], P(('strip', 'tile')), may hold values from -0.25 to 1536.25, as said below
- displacement: float32 [1536, 3, 128], P(('strip', 'tile')), may hold values from -0.75 to 0.75
- pairs: int32 [2048, 2], P(('strip', 'tile')), may hold values from 0 to 1535, as said below
- intact: int32 [2048, 128, 128], P(('strip', 'tile')), may hold values 0 or 1
Outputs:
- force: float32 [1536, 3, 128], P(('strip', 'tile'))
Inputs may be any that keep to these rules, and one draw needn't show every extreme that they name: `coords`: each point sits within 0.25 of its lattice site: tile t covers a 4 x 4 x 8 block of unit lattice sites starting at (4 (t // 384), 4 (t % 384), 0), point i at offset (i % 4, (i // 4) % 4, i // 16). `pairs`: the rows of one device (device number d = strip index * 8 + tile index) name as first tile one of the 48 tiles that this device holds, and as second tile a different one whose strip differs from the first's by at most one and whose place within its strip differs from the first's place within its strip by at most one.
All inputs are finite; a program needn't handle non-finite values. No bound on the sum of `intact` on one device may be relied on, other than what follows from the above.
Results may differ from a plain program's by a relative error of at most 0.0003.
Values sent between devices are 32-bit elements; how exact they have to be, the bound alone decides.
A program may use at most 64 MiB of HBM per device.

v0:
```python
import math

import jax
import jax.numpy as jnp
from jax import lax
from jax.sharding import PartitionSpec as P

horizon = 3.0
stiffness = 2.0
onset_stretch = 0.02
final_stretch = 0.05


def from_behind(value, axis, steps):
    count = lax.axis_size(axis)
    first, last = (max(0, -steps), min(count, count - steps))
    return lax.ppermute(value, axis, [(source, source + steps) for source in range(first, last)])


def padded(block, sides, width):
    for axis, dim in sides:
        count = lax.axis_size(axis)
        forward = [(i, i + 1) for i in range(count - 1)]
        backward = [(target, source) for source, target in forward]
        low = lax.ppermute(
            lax.slice_in_dim(block, block.shape[dim] - width, None, axis=dim), axis, forward
        )
        high = lax.ppermute(lax.slice_in_dim(block, 0, width, axis=dim), axis, backward)
        block = jnp.concatenate([low, block, high], axis=dim)
    return block


def block_forces(first_block, second, bond_mask):
    bond_ref = second[0:3, None, :] - first_block[0:3, :, None]
    bond_now = bond_ref + second[3:6, None, :] - first_block[3:6, :, None]
    length_ref = jnp.sqrt(jnp.sum(bond_ref * bond_ref, axis=0))
    length_now = jnp.sqrt(jnp.sum(bond_now * bond_now, axis=0))
    stretch = (length_now - length_ref) / length_ref
    influence = jnp.maximum(0.0, 1.0 - length_ref / horizon)
    soften = jnp.clip((final_stretch - stretch) / (final_stretch - onset_stretch), 0.0, 1.0)
    pull_scale = (
        stiffness * stretch * influence * soften * bond_mask.astype(jnp.float32) / length_now
    )
    bond_force = pull_scale[None] * bond_now
    return (jnp.sum(bond_force, axis=2), -jnp.sum(bond_force, axis=1))


def strip_pass(below_part, above_part):
    from_above = from_behind(below_part, "strip", -1)
    from_below = from_behind(above_part, "strip", 1)
    return from_above + from_below


def tile_pass(left_edge, right_edge):
    to_last = from_behind(left_edge, "tile", -1)
    to_first = from_behind(right_edge, "tile", 1)
    return (to_last, to_first)


def on_device(coords, displacement, pairs, intact):
    owned = jnp.concatenate([coords, displacement], axis=1)
    per_device = owned.shape[0]
    span = per_device + 2
    points = owned.shape[-1]
    strip_tiles = per_device * lax.axis_size("tile")
    framed = padded(owned[None], (("strip", 0), ("tile", 1)), 1)
    framed = framed.reshape(3 * span, 6, points)
    strip_index = lax.axis_index("strip")
    tile_index = lax.axis_index("tile")

    def place(tile_ids):
        row_part = (tile_ids // strip_tiles - strip_index + 1) * span
        return row_part + tile_ids % strip_tiles - tile_index * per_device + 1

    group_size = math.gcd(pairs.shape[0], 8)
    grouped_pairs = pairs.reshape(-1, group_size, 2)
    grouped_bonds = intact.reshape(-1, group_size, intact.shape[1], intact.shape[2])

    def visit(forces, scan_item):
        couple, bond_mask = scan_item
        first_slots = place(couple[:, 0])
        second_slots = place(couple[:, 1])
        gain_first, gain_second = jax.vmap(block_forces)(
            framed[first_slots], framed[second_slots], bond_mask
        )
        forces = forces.at[first_slots].add(gain_first)
        forces = forces.at[second_slots].add(gain_second)
        return (forces, None)

    zero_forces = jnp.zeros((3 * span, 3, points), jnp.float32)
    forces, unused = lax.scan(visit, zero_forces, (grouped_pairs, grouped_bonds))
    buffer = forces.reshape(3, span, 3, points)
    strip_row = buffer[1] + strip_pass(buffer[0], buffer[2])
    to_last, to_first = tile_pass(strip_row[0], strip_row[span - 1])
    result = strip_row[1 : span - 1]
    result = result.at[per_device - 1].add(to_last)
    result = result.at[0].add(to_first)
    return result


def solution(mesh):
    placed = (
        P(("strip", "tile"), None, None),
        P(("strip", "tile"), None, None),
        P(("strip", "tile"), None),
        P(("strip", "tile"), None, None),
    )
    return jax.shard_map(
        on_device,
        mesh=mesh,
        in_specs=placed,
        out_specs=P(("strip", "tile"), None, None),
        check_vma=False,
    )
```

profile of v0, /device:TPU:12, one launch (start us, length us, event | category | flops | bytes accessed | tf_op | source)
XLA Modules:
  0.0 94.7 jit_solution(17413819467108149188)
XLA Ops:
  0.9 3.5 %collective-permute-start = (f32[1,48,6,128]{3,1,2,0:T(8,128)S(1)}, f32[1,48,6,128]{3,1,2,0:T(8,128)S(1)}, u32[]{:S(2)}, u32[]{:S(2)}) collective-permute-start(f32[1,48,6,128]{3,1,2,0:T(8,128)S(1)} %maximum_bitcast_fusion), channel_id=1, source_target_pairs={{0,8},{8,16},{16,24},{1,9},{9,17},{17,25},{2,10},{10,18},{18,26},{... | collective-permute-start | bytes 442376 | tf_op jit(solution)/shard_map/ppermute | solution.py:25
  4.4 2.4 %collective-permute-start.1 = (f32[1,48,6,128]{3,1,2,0:T(8,128)S(1)}, f32[1,48,6,128]{3,1,2,0:T(8,128)S(1)}, u32[]{:S(2)}, u32[]{:S(2)}) collective-permute-start(f32[1,48,6,128]{3,1,2,0:T(8,128)S(1)} %maximum_bitcast_fusion), channel_id=1, source_target_pairs={{8,0},{16,8},{24,16},{9,1},{17,9},{25,17},{10,2},{18,10},{26,18},{... | collective-permute-start | bytes 442376 | tf_op jit(solution)/shard_map/ppermute | solution.py:28
  6.8 1.6 %collective-permute-done = f32[1,48,6,128]{3,1,2,0:T(8,128)S(1)} collective-permute-done((f32[1,48,6,128]{3,1,2,0:T(8,128)S(1)}, f32[1,48,6,128]{3,1,2,0:T(8,128)S(1)}, u32[]{:S(2)}, u32[]{:S(2)}) %collective-permute-start) | collective-permute-done | bytes 147488 | tf_op jit(solution)/shard_map/ppermute | solution.py:25
  8.4 3.2 %collective-permute-done.1 = f32[1,48,6,128]{3,1,2,0:T(8,128)S(1)} collective-permute-done((f32[1,48,6,128]{3,1,2,0:T(8,128)S(1)}, f32[1,48,6,128]{3,1,2,0:T(8,128)S(1)}, u32[]{:S(2)}, u32[]{:S(2)}) %collective-permute-start.1) | collective-permute-done | bytes 147488 | tf_op jit(solution)/shard_map/ppermute | solution.py:28
  11.6 1.9 %collective-permute-start.2 = (f32[3,1,6,128]{3,1,2,0:T(1,128)S(1)}, f32[3,1,6,128]{3,1,2,0:T(1,128)S(1)}, u32[]{:S(2)}, u32[]{:S(2)}) collective-permute-start(f32[3,1,6,128]{3,1,2,0:T(1,128)S(1)} %get-tuple-element.205), channel_id=1, source_target_pairs={{0,1},{1,2},{2,3},{3,4},{4,5},{5,6},{6,7},{8,9},{9,10},{10,11},{11... | collective-permute-start | bytes 27656 | tf_op jit(solution)/shard_map/ppermute | solution.py:25
  13.6 4.5 %collective-permute-start.3 = (f32[3,1,6,128]{3,1,2,0:T(1,128)S(1)}, f32[3,1,6,128]{3,1,2,0:T(1,128)S(1)}, u32[]{:S(2)}, u32[]{:S(2)}) collective-permute-start(f32[3,1,6,128]{3,1,2,0:T(1,128)S(1)} %get-tuple-element.206), channel_id=1, source_target_pairs={{1,0},{2,1},{3,2},{4,3},{5,4},{6,5},{7,6},{9,8},{10,9},{11,10},{12... | collective-permute-start | bytes 27656 | tf_op jit(solution)/shard_map/ppermute | solution.py:28
  19.7 56.3 %while.15 = (s32[]{:T(128)}, f32[150,3,128]{2,1,0:T(4,128)S(1)}, s32[8,8,2]{1,0,2:T(8,128)S(1)}, s32[]{:T(128)}, s32[]{:T(128)}, /*index=5*/f32[150,6,128]{2,1,0:T(8,128)S(1)}, s32[8,8,128,128]{3,2,1,0:T(8,128)}, s32[]{:T(128)}) while((s32[]{:T(128)}, f32[150,3,128]{2,1,0:T(4,128)S(1)}, s32[8,8,2]{1,0,2:T(8,128)S(1)}, s32[]{:T(128)}, ...), condition=%wide.region_7.8_spmd, body=%wide.region_0.7_spmd.sunk | while | flops 6690130 | bytes 4096549 | solution.py:91
  22.0 1.6 %fusion.27 = f32[8,128,128]{2,1,0:T(8,128)S(1)} fusion(s32[8,8,128,128]{3,2,1,0:T(8,128)} %get-tuple-element.300, s32[]{:T(128)} %get-tuple-element.286, f32[8,128,128]{2,1,0:T(8,128)S(1)} %get-tuple-element.274, f32[8,128,128]{2,1,0:T(8,128)S(1)} %get-tuple-element.275), kind=kLoop, calls=%fused_computation.15.clone.1 | loop fusion | flops 1835008 | bytes 2097156 | tf_op jit(solution)/shard_map/while/body/eval_jaxpr/vmap()/div | solution.py:42
  23.6 1.6 %fusion.28 = (f32[8,3,128]{2,1,0:T(4,128)S(1)}, f32[8,3,128]{2,1,0:T(4,128)S(1)}) fusion(f32[8,128,128]{2,1,0:T(8,128)S(1)} %fusion.27, f32[8,3,128]{2,1,0:T(4,128)S(1)} %get-tuple-element.269, f32[8,3,128]{2,1,0:T(4,128)S(1)} %get-tuple-element.271, f32[8,3,128]{2,1,0:T(4,128)S(1)} %get-tuple-element.272, f32[8,3,128]{2,1,0:T(4,128)S(1)} %get-tuple-element.273), kind=kLoop, calls=%fused_computation.9.clone.1 | loop fusion | flops 2353152 | bytes 598016 | tf_op jit(solution)/shard_map/while/body/eval_jaxpr/vmap()/reduce_sum | solution.py:45
  29.0 1.6 %fusion.27 = f32[8,128,128]{2,1,0:T(8,128)S(1)} fusion(s32[8,8,128,128]{3,2,1,0:T(8,128)} %get-tuple-element.300, s32[]{:T(128)} %get-tuple-element.286, f32[8,128,128]{2,1,0:T(8,128)S(1)} %get-tuple-element.274, f32[8,128,128]{2,1,0:T(8,128)S(1)} %get-tuple-element.275), kind=kLoop, calls=%fused_computation.15.clone.1 | loop fusion | flops 1835008 | bytes 2097156 | tf_op jit(solution)/shard_map/while/body/eval_jaxpr/vmap()/div | solution.py:42
  30.6 1.6 %fusion.28 = (f32[8,3,128]{2,1,0:T(4,128)S(1)}, f32[8,3,128]{2,1,0:T(4,128)S(1)}) fusion(f32[8,128,128]{2,1,0:T(8,128)S(1)} %fusion.27, f32[8,3,128]{2,1,0:T(4,128)S(1)} %get-tuple-element.269, f32[8,3,128]{2,1,0:T(4,128)S(1)} %get-tuple-element.271, f32[8,3,128]{2,1,0:T(4,128)S(1)} %get-tuple-element.272, f32[8,3,128]{2,1,0:T(4,128)S(1)} %get-tuple-element.273), kind=kLoop, calls=%fused_computation.9.clone.1 | loop fusion | flops 2353152 | bytes 598016 | tf_op jit(solution)/shard_map/while/body/eval_jaxpr/vmap()/reduce_sum | solution.py:45
  35.0 1.0 %fusion.26 = (f32[8,128,128]{2,1,0:T(8,128)S(1)}, f32[8,128,128]{2,1,0:T(8,128)S(1)}) fusion(f32[8,3,128]{2,1,0:T(4,128)S(1)} %get-tuple-element.269, f32[8,3,128]{2,1,0:T(4,128)S(1)} %get-tuple-element.271, f32[8,3,128]{2,1,0:T(4,128)S(1)} %get-tuple-element.272, f32[8,3,128]{2,1,0:T(4,128)S(1)} %get-tuple-element.273), kind=kLoop, calls=%fused_computation.11.clone.1 | loop fusion | flops 2490368 | bytes 1097728 | tf_op jit(solution)/shard_map/while/body/eval_jaxpr/vmap()/reduce_sum | solution.py:37
  36.1 1.6 %fusion.27 = f32[8,128,128]{2,1,0:T(8,128)S(1)} fusion(s32[8,8,128,128]{3,2,1,0:T(8,128)} %get-tuple-element.300, s32[]{:T(128)} %get-tuple-element.286, f32[8,128,128]{2,1,0:T(8,128)S(1)} %get-tuple-element.274, f32[8,128,128]{2,1,0:T(8,128)S(1)} %get-tuple-element.275), kind=kLoop, calls=%fused_computation.15.clone.1 | loop fusion | flops 1835008 | bytes 2097156 | tf_op jit(solution)/shard_map/while/body/eval_jaxpr/vmap()/div | solution.py:42
  37.7 1.6 %fusion.28 = (f32[8,3,128]{2,1,0:T(4,128)S(1)}, f32[8,3,128]{2,1,0:T(4,128)S(1)}) fusion(f32[8,128,128]{2,1,0:T(8,128)S(1)} %fusion.27, f32[8,3,128]{2,1,0:T(4,128)S(1)} %get-tuple-element.269, f32[8,3,128]{2,1,0:T(4,128)S(1)} %get-tuple-element.271, f32[8,3,128]{2,1,0:T(4,128)S(1)} %get-tuple-element.272, f32[8,3,128]{2,1,0:T(4,128)S(1)} %get-tuple-element.273), kind=kLoop, calls=%fused_computation.9.clone.1 | loop fusion | flops 2353152 | bytes 598016 | tf_op jit(solution)/shard_map/while/body/eval_jaxpr/vmap()/reduce_sum | solution.py:45
  43.1 1.6 %fusion.27 = f32[8,128,128]{2,1,0:T(8,128)S(1)} fusion(s32[8,8,128,128]{3,2,1,0:T(8,128)} %get-tuple-element.300, s32[]{:T(128)} %get-tuple-element.286, f32[8,128,128]{2,1,0:T(8,128)S(1)} %get-tuple-element.274, f32[8,128,128]{2,1,0:T(8,128)S(1)} %get-tuple-element.275), kind=kLoop, calls=%fused_computation.15.clone.1 | loop fusion | flops 1835008 | bytes 2097156 | tf_op jit(solution)/shard_map/while/body/eval_jaxpr/vmap()/div | solution.py:42
  44.7 1.6 %fusion.28 = (f32[8,3,128]{2,1,0:T(4,128)S(1)}, f32[8,3,128]{2,1,0:T(4,128)S(1)}) fusion(f32[8,128,128]{2,1,0:T(8,128)S(1)} %fusion.27, f32[8,3,128]{2,1,0:T(4,128)S(1)} %get-tuple-element.269, f32[8,3,128]{2,1,0:T(4,128)S(1)} %get-tuple-element.271, f32[8,3,128]{2,1,0:T(4,128)S(1)} %get-tuple-element.272, f32[8,3,128]{2,1,0:T(4,128)S(1)} %get-tuple-element.273), kind=kLoop, calls=%fused_computation.9.clone.1 | loop fusion | flops 2353152 | bytes 598016 | tf_op jit(solution)/shard_map/while/body/eval_jaxpr/vmap()/reduce_sum | solution.py:45
  50.2 1.6 %fusion.27 = f32[8,128,128]{2,1,0:T(8,128)S(1)} fusion(s32[8,8,128,128]{3,2,1,0:T(8,128)} %get-tuple-element.300, s32[]{:T(128)} %get-tuple-element.286, f32[8,128,128]{2,1,0:T(8,128)S(1)} %get-tuple-element.274, f32[8,128,128]{2,1,0:T(8,128)S(1)} %get-tuple-element.275), kind=kLoop, calls=%fused_computation.15.clone.1 | loop fusion | flops 1835008 | bytes 2097156 | tf_op jit(solution)/shard_map/while/body/eval_jaxpr/vmap()/div | solution.py:42
  51.7 1.6 %fusion.28 = (f32[8,3,128]{2,1,0:T(4,128)S(1)}, f32[8,3,128]{2,1,0:T(4,128)S(1)}) fusion(f32[8,128,128]{2,1,0:T(8,128)S(1)} %fusion.27, f32[8,3,128]{2,1,0:T(4,128)S(1)} %get-tuple-element.269, f32[8,3,128]{2,1,0:T(4,128)S(1)} %get-tuple-element.271, f32[8,3,128]{2,1,0:T(4,128)S(1)} %get-tuple-element.272, f32[8,3,128]{2,1,0:T(4,128)S(1)} %get-tuple-element.273), kind=kLoop, calls=%fused_computation.9.clone.1 | loop fusion | flops 2353152 | bytes 598016 | tf_op jit(solution)/shard_map/while/body/eval_jaxpr/vmap()/reduce_sum | solution.py:45
  56.2 1.0 %fusion.26 = (f32[8,128,128]{2,1,0:T(8,128)S(1)}, f32[8,128,128]{2,1,0:T(8,128)S(1)}) fusion(f32[8,3,128]{2,1,0:T(4,128)S(1)} %get-tuple-element.269, f32[8,3,128]{2,1,0:T(4,128)S(1)} %get-tuple-element.271, f32[8,3,128]{2,1,0:T(4,128)S(1)} %get-tuple-element.272, f32[8,3,128]{2,1,0:T(4,128)S(1)} %get-tuple-element.273), kind=kLoop, calls=%fused_computation.11.clone.1 | loop fusion | flops 2490368 | bytes 1097728 | tf_op jit(solution)/shard_map/while/body/eval_jaxpr/vmap()/reduce_sum | solution.py:37
  57.2 1.6 %fusion.27 = f32[8,128,128]{2,1,0:T(8,128)S(1)} fusion(s32[8,8,128,128]{3,2,1,0:T(8,128)} %get-tuple-element.300, s32[]{:T(128)} %get-tuple-element.286, f32[8,128,128]{2,1,0:T(8,128)S(1)} %get-tuple-element.274, f32[8,128,128]{2,1,0:T(8,128)S(1)} %get-tuple-element.275), kind=kLoop, calls=%fused_computation.15.clone.1 | loop fusion | flops 1835008 | bytes 2097156 | tf_op jit(solution)/shard_map/while/body/eval_jaxpr/vmap()/div | solution.py:42
  58.8 1.6 %fusion.28 = (f32[8,3,128]{2,1,0:T(4,128)S(1)}, f32[8,3,128]{2,1,0:T(4,128)S(1)}) fusion(f32[8,128,128]{2,1,0:T(8,128)S(1)} %fusion.27, f32[8,3,128]{2,1,0:T(4,128)S(1)} %get-tuple-element.269, f32[8,3,128]{2,1,0:T(4,128)S(1)} %get-tuple-element.271, f32[8,3,128]{2,1,0:T(4,128)S(1)} %get-tuple-element.272, f32[8,3,128]{2,1,0:T(4,128)S(1)} %get-tuple-element.273), kind=kLoop, calls=%fused_computation.9.clone.1 | loop fusion | flops 2353152 | bytes 598016 | tf_op jit(solution)/shard_map/while/body/eval_jaxpr/vmap()/reduce_sum | solution.py:45
  64.3 1.6 %fusion.27 = f32[8,128,128]{2,1,0:T(8,128)S(1)} fusion(s32[8,8,128,128]{3,2,1,0:T(8,128)} %get-tuple-element.300, s32[]{:T(128)} %get-tuple-element.286, f32[8,128,128]{2,1,0:T(8,128)S(1)} %get-tuple-element.274, f32[8,128,128]{2,1,0:T(8,128)S(1)} %get-tuple-element.275), kind=kLoop, calls=%fused_computation.15.clone.1 | loop fusion | flops 1835008 | bytes 2097156 | tf_op jit(solution)/shard_map/while/body/eval_jaxpr/vmap()/div | solution.py:42
  65.8 1.6 %fusion.28 = (f32[8,3,128]{2,1,0:T(4,128)S(1)}, f32[8,3,128]{2,1,0:T(4,128)S(1)}) fusion(f32[8,128,128]{2,1,0:T(8,128)S(1)} %fusion.27, f32[8,3,128]{2,1,0:T(4,128)S(1)} %get-tuple-element.269, f32[8,3,128]{2,1,0:T(4,128)S(1)} %get-tuple-element.271, f32[8,3,128]{2,1,0:T(4,128)S(1)} %get-tuple-element.272, f32[8,3,128]{2,1,0:T(4,128)S(1)} %get-tuple-element.273), kind=kLoop, calls=%fused_computation.9.clone.1 | loop fusion | flops 2353152 | bytes 598016 | tf_op jit(solution)/shard_map/while/body/eval_jaxpr/vmap()/reduce_sum | solution.py:45
  71.3 1.6 %fusion.27 = f32[8,128,128]{2,1,0:T(8,128)S(1)} fusion(s32[8,8,128,128]{3,2,1,0:T(8,128)} %get-tuple-element.300, s32[]{:T(128)} %get-tuple-element.286, f32[8,128,128]{2,1,0:T(8,128)S(1)} %get-tuple-element.274, f32[8,128,128]{2,1,0:T(8,128)S(1)} %get-tuple-element.275), kind=kLoop, calls=%fused_computation.15.clone.1 | loop fusion | flops 1835008 | bytes 2097156 | tf_op jit(solution)/shard_map/while/body/eval_jaxpr/vmap()/div | solution.py:42
  72.9 1.6 %fusion.28 = (f32[8,3,128]{2,1,0:T(4,128)S(1)}, f32[8,3,128]{2,1,0:T(4,128)S(1)}) fusion(f32[8,128,128]{2,1,0:T(8,128)S(1)} %fusion.27, f32[8,3,128]{2,1,0:T(4,128)S(1)} %get-tuple-element.269, f32[8,3,128]{2,1,0:T(4,128)S(1)} %get-tuple-element.271, f32[8,3,128]{2,1,0:T(4,128)S(1)} %get-tuple-element.272, f32[8,3,128]{2,1,0:T(4,128)S(1)} %get-tuple-element.273), kind=kLoop, calls=%fused_computation.9.clone.1 | loop fusion | flops 2353152 | bytes 598016 | tf_op jit(solution)/shard_map/while/body/eval_jaxpr/vmap()/reduce_sum | solution.py:45
  76.1 2.4 %collective-permute-start.4 = (f32[50,3,128]{2,1,0:T(4,128)S(1)}, f32[50,3,128]{2,1,0:T(4,128)S(1)}, u32[]{:S(2)}, u32[]{:S(2)}) collective-permute-start(f32[50,3,128]{2,1,0:T(4,128)S(1)} %get-tuple-element.208), channel_id=1, source_target_pairs={{8,0},{16,8},{24,16},{9,1},{17,9},{25,17},{10,2},{18,10},{26,18},{... | collective-permute-start | bytes 230408 | tf_op jit(solution)/shard_map/ppermute | solution.py:17
  78.5 3.5 %collective-permute-start.5 = (f32[50,3,128]{2,1,0:T(4,128)S(1)}, f32[50,3,128]{2,1,0:T(4,128)S(1)}, u32[]{:S(2)}, u32[]{:S(2)}) collective-permute-start(f32[50,3,128]{2,1,0:T(4,128)S(1)} %get-tuple-element.207), channel_id=1, source_target_pairs={{0,8},{8,16},{16,24},{1,9},{9,17},{17,25},{2,10},{10,18},{18,26},{... | collective-permute-start | bytes 230408 | tf_op jit(solution)/shard_map/ppermute | solution.py:17
  82.0 1.5 %collective-permute-done.4 = f32[50,3,128]{2,1,0:T(4,128)S(1)} collective-permute-done((f32[50,3,128]{2,1,0:T(4,128)S(1)}, f32[50,3,128]{2,1,0:T(4,128)S(1)}, u32[]{:S(2)}, u32[]{:S(2)}) %collective-permute-start.4) | collective-permute-done | bytes 76832 | tf_op jit(solution)/shard_map/ppermute | solution.py:17
  83.5 2.1 %collective-permute-done.5 = f32[50,3,128]{2,1,0:T(4,128)S(1)} collective-permute-done((f32[50,3,128]{2,1,0:T(4,128)S(1)}, f32[50,3,128]{2,1,0:T(4,128)S(1)}, u32[]{:S(2)}, u32[]{:S(2)}) %collective-permute-start.5) | collective-permute-done | bytes 76832 | tf_op jit(solution)/shard_map/ppermute | solution.py:17
  85.6 2.6 %collective-permute-start.6 = (f32[3,128]{1,0:T(4,128)S(1)}, f32[3,128]{1,0:T(4,128)S(1)}, u32[]{:S(2)}, u32[]{:S(2)}) collective-permute-start(f32[3,128]{1,0:T(4,128)S(1)} %get-tuple-element.210), channel_id=1, source_target_pairs={{1,0},{2,1},{3,2},{4,3},{5,4},{6,5},{7,6},{9,8},{10,9},{11,10},{12... | collective-permute-start | bytes 4616 | tf_op jit(solution)/shard_map/ppermute | solution.py:17
  88.2 1.9 %collective-permute-start.7 = (f32[3,128]{1,0:T(4,128)S(1)}, f32[3,128]{1,0:T(4,128)S(1)}, u32[]{:S(2)}, u32[]{:S(2)}) collective-permute-start(f32[3,128]{1,0:T(4,128)S(1)} %get-tuple-element.209), channel_id=1, source_target_pairs={{0,1},{1,2},{2,3},{3,4},{4,5},{5,6},{6,7},{8,9},{9,10},{10,11},{11... | collective-permute-start | bytes 4616 | tf_op jit(solution)/shard_map/ppermute | solution.py:17
  90.2 3.9 %collective-permute-done.7 = f32[3,128]{1,0:T(4,128)S(1)} collective-permute-done((f32[3,128]{1,0:T(4,128)S(1)}, f32[3,128]{1,0:T(4,128)S(1)}, u32[]{:S(2)}, u32[]{:S(2)}) %collective-permute-start.7) | collective-permute-done | bytes 1568 | tf_op jit(solution)/shard_map/ppermute | solution.py:17
  (102 shorter events, 31.4 us)
Async XLA Ops:
  0.9 7.5 %collective-permute-start = (f32[1,48,6,128]{3,1,2,0:T(8,128)S(1)}, f32[1,48,6,128]{3,1,2,0:T(8,128)S(1)}, u32[]{:S(2)}, u32[]{:S(2)}) collective-permute-start(f32[1,48,6,128]{3,1,2,0:T(8,128)S(1)} %maximum_bitcast_fusion), channel_id=1, source_target_pairs={{0,8},{8,16},{16,24},{1,9},{9,17},{17,25},{2,10},{10,18},{18,26},{... | collective-permute-start | bytes 442376 | tf_op jit(solution)/shard_map/ppermute | solution.py:25
  4.4 7.2 %collective-permute-start.1 = (f32[1,48,6,128]{3,1,2,0:T(8,128)S(1)}, f32[1,48,6,128]{3,1,2,0:T(8,128)S(1)}, u32[]{:S(2)}, u32[]{:S(2)}) collective-permute-start(f32[1,48,6,128]{3,1,2,0:T(8,128)S(1)} %maximum_bitcast_fusion), channel_id=1, source_target_pairs={{8,0},{16,8},{24,16},{9,1},{17,9},{25,17},{10,2},{18,10},{26,18},{... | collective-permute-start | bytes 442376 | tf_op jit(solution)/shard_map/ppermute | solution.py:28
  11.6 7.2 %collective-permute-start.2 = (f32[3,1,6,128]{3,1,2,0:T(1,128)S(1)}, f32[3,1,6,128]{3,1,2,0:T(1,128)S(1)}, u32[]{:S(2)}, u32[]{:S(2)}) collective-permute-start(f32[3,1,6,128]{3,1,2,0:T(1,128)S(1)} %get-tuple-element.205), channel_id=1, source_target_pairs={{0,1},{1,2},{2,3},{3,4},{4,5},{5,6},{6,7},{8,9},{9,10},{10,11},{11... | collective-permute-start | bytes 27656 | tf_op jit(solution)/shard_map/ppermute | solution.py:25
  13.6 5.9 %collective-permute-start.3 = (f32[3,1,6,128]{3,1,2,0:T(1,128)S(1)}, f32[3,1,6,128]{3,1,2,0:T(1,128)S(1)}, u32[]{:S(2)}, u32[]{:S(2)}) collective-permute-start(f32[3,1,6,128]{3,1,2,0:T(1,128)S(1)} %get-tuple-element.206), channel_id=1, source_target_pairs={{1,0},{2,1},{3,2},{4,3},{5,4},{6,5},{7,6},{9,8},{10,9},{11,10},{12... | collective-permute-start | bytes 27656 | tf_op jit(solution)/shard_map/ppermute | solution.py:28
  76.1 7.4 %collective-permute-start.4 = (f32[50,3,128]{2,1,0:T(4,128)S(1)}, f32[50,3,128]{2,1,0:T(4,128)S(1)}, u32[]{:S(2)}, u32[]{:S(2)}) collective-permute-start(f32[50,3,128]{2,1,0:T(4,128)S(1)} %get-tuple-element.208), channel_id=1, source_target_pairs={{8,0},{16,8},{24,16},{9,1},{17,9},{25,17},{10,2},{18,10},{26,18},{... | collective-permute-start | bytes 230408 | tf_op jit(solution)/shard_map/ppermute | solution.py:17
  78.5 7.1 %collective-permute-start.5 = (f32[50,3,128]{2,1,0:T(4,128)S(1)}, f32[50,3,128]{2,1,0:T(4,128)S(1)}, u32[]{:S(2)}, u32[]{:S(2)}) collective-permute-start(f32[50,3,128]{2,1,0:T(4,128)S(1)} %get-tuple-element.207), channel_id=1, source_target_pairs={{0,8},{8,16},{16,24},{1,9},{9,17},{17,25},{2,10},{10,18},{18,26},{... | collective-permute-start | bytes 230408 | tf_op jit(solution)/shard_map/ppermute | solution.py:17
  85.6 4.5 %collective-permute-start.6 = (f32[3,128]{1,0:T(4,128)S(1)}, f32[3,128]{1,0:T(4,128)S(1)}, u32[]{:S(2)}, u32[]{:S(2)}) collective-permute-start(f32[3,128]{1,0:T(4,128)S(1)} %get-tuple-element.210), channel_id=1, source_target_pairs={{1,0},{2,1},{3,2},{4,3},{5,4},{6,5},{7,6},{9,8},{10,9},{11,10},{12... | collective-permute-start | bytes 4616 | tf_op jit(solution)/shard_map/ppermute | solution.py:17
  88.2 5.8 %collective-permute-start.7 = (f32[3,128]{1,0:T(4,128)S(1)}, f32[3,128]{1,0:T(4,128)S(1)}, u32[]{:S(2)}, u32[]{:S(2)}) collective-permute-start(f32[3,128]{1,0:T(4,128)S(1)} %get-tuple-element.209), channel_id=1, source_target_pairs={{0,1},{1,2},{2,3},{3,4},{4,5},{5,6},{6,7},{8,9},{9,10},{10,11},{11... | collective-permute-start | bytes 4616 | tf_op jit(solution)/shard_map/ppermute | solution.py:17
where the time goes:
time: 95.4 us; the launch traced here: 94.7 us
  other arithmetic  47.5 us (50%)
  starting transfers between devices  22.6 us (24%)
  waiting for transfers between devices  12.9 us (14%)
  local copies, waits for them, and re-layouts  10.7 us (11%)
    reduce_sum x8, other arithmetic, block_forces(): return (jnp.sum(bond_force, axis=2), -jnp.sum(bond_force, axis=1))  12.8 us
    div x8, other arithmetic, block_forces(): stiffness * stretch * influence * soften * bond_mask.astype(jnp.float32)  12.5 us
    ppermute x4, starting transfers between devices, from_behind(): lax.ppermute(value, axis, [(source, source + steps) for source in range(f...  10.3 us
    reduce_sum x8, other arithmetic, block_forces(): length_now = jnp.sqrt(jnp.sum(bond_now * bond_now, axis=0))  8.37 us
    ppermute x4, waiting for transfers between devices, from_behind(): lax.ppermute(value, axis, [(source, source + steps) for source in range(f...  7.44 us
    ppermute x2, starting transfers between devices, padded(): lax.ppermute(lax.slice_in_dim(block, 0, width, axis=dim), axis, backward)  6.9 us
    scatter-add x8, other arithmetic, visit(): forces = forces.at[first_slots].add(gain_first)  6.24 us
    scatter-add x8, other arithmetic, visit(): forces = forces.at[second_slots].add(gain_second)  6.23 us
  transfers between devices with their start and end apart: 8, of which 6 were waited for; matrix products, arithmetic and copies ran while one was open for 1% of the time, Pallas kernels for 0%

commit v1 on v0

v1 whole, which is shorter than its diff:
```python
import math

import jax
import jax.numpy as jnp
from jax import lax
from jax.experimental import pallas as pl
from jax.experimental.pallas import tpu as pltpu
from jax.sharding import PartitionSpec as P

horizon = 3.0
stiffness = 2.0
onset_stretch = 0.02
final_stretch = 0.05


def from_behind(value, axis, steps):
    count = lax.axis_size(axis)
    first, last = (max(0, -steps), min(count, count - steps))
    return lax.ppermute(value, axis, [(source, source + steps) for source in range(first, last)])


def padded(block, sides, width):
    for axis, dim in sides:
        count = lax.axis_size(axis)
        forward = [(i, i + 1) for i in range(count - 1)]
        backward = [(target, source) for source, target in forward]
        low = lax.ppermute(
            lax.slice_in_dim(block, block.shape[dim] - width, None, axis=dim), axis, forward
        )
        high = lax.ppermute(lax.slice_in_dim(block, 0, width, axis=dim), axis, backward)
        block = jnp.concatenate([low, block, high], axis=dim)
    return block


def strip_pass(below_part, above_part):
    from_above = from_behind(below_part, "strip", -1)
    from_below = from_behind(above_part, "strip", 1)
    return from_above + from_below


def tile_pass(left_edge, right_edge):
    to_last = from_behind(left_edge, "tile", -1)
    to_first = from_behind(right_edge, "tile", 1)
    return (to_last, to_first)


def split_rows(rows):
    row = lax.broadcasted_iota(jnp.int32, rows.shape, 0)
    lead = jnp.where(row < 3, rows, jnp.where(row == 3, 1.0, 0.0))
    high = lead.astype(jnp.bfloat16).astype(jnp.float32)
    return jnp.concatenate([high, lead - high], axis=0).astype(jnp.bfloat16)


def pair_pull(first_columns, second_rows, shift, bonds):
    def part(c):
        return second_rows[c : c + 1] + shift[c] - first_columns[:, c : c + 1]

    def norm2(c):
        x, y, z = part(c), part(c + 1), part(c + 2)
        return x * x + y * y + z * z

    now2, ref2 = norm2(0), norm2(3)
    inv_now, inv_ref = lax.rsqrt(now2), lax.rsqrt(ref2)
    ratio = now2 * inv_now * inv_ref
    influence = jnp.maximum(0.0, stiffness - ref2 * inv_ref * (stiffness / horizon))
    span = final_stretch - onset_stretch
    soften = jnp.clip((1.0 + final_stretch - ratio) * (1.0 / span), 0.0, 1.0)
    pull = (ratio - 1.0) * influence * (soften * inv_now)
    return jnp.where(bonds != 0, pull, 0.0)


def dot_rows(rows, matrix):
    return lax.dot_general(rows, matrix, (((1,), (0,)), ((), ())), preferred_element_type=jnp.float32)


def dot_columns(rows, matrix):
    return lax.dot_general(rows, matrix, (((1,), (1,)), ((), ())), preferred_element_type=jnp.float32)


def forces_kernel(group, chunk, slots_ref, table_ref, bonds_ref, forces_ref):
    step = pl.program_id(0)
    points = table_ref.shape[2]

    @pl.when(step == 0)
    def _():
        forces_ref[...] = jnp.zeros_like(forces_ref)

    def visit(i, carry):
        k = step * group + i
        first, second = slots_ref[0, k], slots_ref[1, k]
        move_x = slots_ref[2, k].astype(jnp.float32)
        move_y = slots_ref[3, k].astype(jnp.float32)
        first_rows, second_rows = table_ref[first], table_ref[second]
        shift = (move_x, move_y, 0.0, move_x, move_y, 0.0)
        columns = first_rows.T
        leads, rests = [], []
        for at in range(0, points, chunk):
            pull = pair_pull(
                columns[at : at + chunk], second_rows, shift, bonds_ref[i, at : at + chunk]
            )
            lead = pull.astype(jnp.bfloat16)
            leads.append(lead)
            rests.append((pull - lead.astype(jnp.float32)).astype(jnp.bfloat16))
        lead, rest = jnp.concatenate(leads, axis=0), jnp.concatenate(rests, axis=0)
        first_split, second_split = split_rows(first_rows), split_rows(second_rows)
        to_first = dot_columns(second_split, lead) + dot_columns(second_split, rest)
        to_second = dot_rows(first_split, lead) + dot_rows(first_split, rest)
        to_first = to_first[:8] + to_first[8:]
        to_second = to_second[:8] + to_second[8:]
        row = lax.broadcasted_iota(jnp.int32, first_rows.shape, 0)
        move = jnp.where(row == 0, move_x, jnp.where(row == 1, move_y, 0.0))
        forces_ref[first] += to_first - (first_rows - move) * to_first[3:4]
        forces_ref[second] += to_second - (second_rows + move) * to_second[3:4]
        return carry

    lax.fori_loop(0, group, visit, 0, unroll=2)


def pair_forces(slots, table, intact):
    group = math.gcd(intact.shape[0], 8)
    chunk = math.gcd(intact.shape[1], 32)
    return pl.pallas_call(
        lambda *refs: forces_kernel(group, chunk, *refs),
        grid_spec=pltpu.PrefetchScalarGridSpec(
            num_scalar_prefetch=1,
            grid=(intact.shape[0] // group,),
            in_specs=[
                pl.BlockSpec(table.shape, lambda s, slots: (0, 0, 0)),
                pl.BlockSpec((group,) + intact.shape[1:], lambda s, slots: (s, 0, 0)),
            ],
            out_specs=pl.BlockSpec(table.shape, lambda s, slots: (0, 0, 0)),
        ),
        out_shape=jax.ShapeDtypeStruct(table.shape, jnp.float32),
    )(slots, table, intact)


def on_device(coords, displacement, pairs, intact):
    per_device = coords.shape[0]
    span = per_device + 2
    points = coords.shape[-1]
    strip_tiles = per_device * lax.axis_size("tile")
    strip_index = lax.axis_index("strip")
    tile_index = lax.axis_index("tile")
    own_tiles = tile_index * per_device + jnp.arange(per_device)
    origin = jnp.stack(
        [
            jnp.full((per_device,), 4 * strip_index, jnp.int32) + 0 * own_tiles,
            4 * own_tiles,
            0 * own_tiles,
        ],
        axis=1,
    ).astype(jnp.float32)[:, :, None]
    middle = jnp.array([1.5, 1.5, 3.5], jnp.float32)[None, :, None]
    local = coords - origin - middle
    now = local + displacement
    owned = jnp.concatenate(
        [now, local, jnp.zeros((per_device, 2, points), jnp.float32)], axis=1
    )
    framed = padded(owned[None], (("strip", 0), ("tile", 1)), 1)
    framed = framed.reshape(3 * span, 8, points)
    strip_of, place_of = pairs // strip_tiles, pairs % strip_tiles
    slot = (strip_of - strip_index + 1) * span + place_of - tile_index * per_device + 1
    slots = jnp.stack(
        [
            slot[:, 0],
            slot[:, 1],
            4 * (strip_of[:, 1] - strip_of[:, 0]),
            4 * (place_of[:, 1] - place_of[:, 0]),
        ]
    )
    forces = pair_forces(slots, framed, intact)[:, :3]
    buffer = forces.reshape(3, span, 3, points)
    strip_row = buffer[1] + strip_pass(buffer[0], buffer[2])
    to_last, to_first = tile_pass(strip_row[0], strip_row[span - 1])
    result = strip_row[1 : span - 1]
    result = result.at[per_device - 1].add(to_last)
    result = result.at[0].add(to_first)
    return result


def solution(mesh):
    placed = (
        P(("strip", "tile"), None, None),
        P(("strip", "tile"), None, None),
        P(("strip", "tile"), None),
        P(("strip", "tile"), None, None),
    )
    return jax.shard_map(
        on_device,
        mesh=mesh,
        in_specs=placed,
        out_specs=P(("strip", "tile"), None, None),
        check_vma=False,
    )
```

time: 95.4 us -> 67.9 us (0.71)
  other arithmetic: 47.5 us -> 3.58 us
  Pallas kernels: 0 us -> 24.9 us
  local copies, waits for them, and re-layouts: 10.7 us -> 2.81 us
    pallas_call x0 -> x1, Pallas kernels: none -> 24.9 us  [pair_forces(): pl.pallas_call(lambda *refs: forces_kernel(group, chunk, *refs), grid_spe...]
    reduce_sum x16 -> x0, other arithmetic: 21.1 us -> none  [the longest x8 12.8 us: block_forces(): return (jnp.sum(bond_force, axis=2), -jnp.sum(bond_force, axis=1))]
    div x8 -> x0, other arithmetic: 12.5 us -> none  [block_forces(): stiffness * stretch * influence * soften * bond_mask.astype(jnp.float32)]
    scatter-add x16 -> x0, other arithmetic: 12.5 us -> none  [the longest x8 6.24 us: visit(): forces = forces.at[first_slots].add(gain_first)]
    gather x16 -> x0, local copies, waits for them, and re-layouts: 8.88 us -> none  [the longest x8 4.44 us: visit(): framed[first_slots]]
    add x0 -> x2, other arithmetic: none -> 1.73 us  [the longest x1 1.03 us: on_device(): now = local + displacement]
    slice x1, local copies, waits for them, and re-layouts: 0.04 us -> 1.06 us  [on_device(): strip_row = buffer[1] + strip_pass(buffer[0], buffer[2])]
  transfers between devices with their start and end apart: 8 -> 8, of which waited for: 6 -> 6; matrix products, arithmetic and copies ran while one was open for 1% -> 2% of each run, Pallas kernels for 0% -> 0%
where the time goes in v1:
time: 67.9 us; the launch traced here: 67.5 us
  Pallas kernels  24.9 us (37%)
  starting transfers between devices  22.6 us (33%)
  waiting for transfers between devices  13.4 us (20%)
  other arithmetic  3.58 us (5%)
  local copies, waits for them, and re-layouts  2.81 us (4%)
    pallas_call x1, Pallas kernels, pair_forces(): pl.pallas_call(lambda *refs: forces_kernel(group, chunk, *refs), grid_spe...  24.9 us
    ppermute x4, starting transfers between devices, from_behind(): lax.ppermute(value, axis, [(source, source + steps) for source in range(f...  10.3 us
    ppermute x4, waiting for transfers between devices, from_behind(): lax.ppermute(value, axis, [(source, source + steps) for source in range(f...  7.45 us
    ppermute x2, starting transfers between devices, padded(): lax.ppermute(lax.slice_in_dim(block, 0, width, axis=dim), axis, backward)  6.91 us
    ppermute x2, starting transfers between devices, padded(): lax.ppermute(lax.slice_in_dim(block, block.shape[dim] - width, None, axis...  5.41 us
    ppermute x2, waiting for transfers between devices, padded(): lax.ppermute(lax.slice_in_dim(block, 0, width, axis=dim), axis, backward)  4 us
    ppermute x2, waiting for transfers between devices, padded(): lax.ppermute(lax.slice_in_dim(block, block.shape[dim] - width, None, axis...  1.94 us
  transfers between devices with their start and end apart: 8, of which 6 were waited for; matrix products, arithmetic and copies ran while one was open for 2% of the time, Pallas kernels for 0%

profile of v1, /device:TPU:12, one launch (start us, length us, event | category | flops | bytes accessed | tf_op | source)
XLA Modules:
  0.0 67.5 jit_solution(5938058715385062966)
XLA Ops:
  0.0 0.1 pad.17.clone
  0.1 0.1 pad.14.clone
  0.2 0.1 add_convert_fusion
  0.2 1.0 %fusion.2 = (f32[48,3,128]{2,0,1:T(8,128)S(1)}, f32[48,3,128]{2,0,1:T(8,128)S(1)}) fusion(f32[48,3,128]{2,0,1:T(8,128)} %param.10, f32[3]{0:T(128)} %constant.99, f32[48,3,128]{2,0,1:T(8,128)} %param.9, f32[48,3]{0,1:T(4,128)S(1)} %add_convert_fusion), kind=kLoop, calls=%fused_computation.24 | loop fusion | flops 55296 | bytes 295500 | tf_op jit(solution)/shard_map/add | solution.py:155
  1.3 0.1 maximum_bitcast_fusion
  1.4 3.5 %collective-permute-start = (f32[1,48,8,128]{3,1,2,0:T(8,128)S(1)}, f32[1,48,8,128]{3,1,2,0:T(8,128)S(1)}, u32[]{:S(2)}, u32[]{:S(2)}) collective-permute-start(f32[1,48,8,128]{3,1,2,0:T(8,128)S(1)} %maximum_bitcast_fusion), channel_id=1, source_target_pairs={{0,8},{8,16},{16,24},{1,9},{9,17},{17,25},{2,10},{10,18},{18,26},{... | collective-permute-start | bytes 589832 | tf_op jit(solution)/shard_map/ppermute | solution.py:27
  4.9 2.4 %collective-permute-start.1 = (f32[1,48,8,128]{3,1,2,0:T(8,128)S(1)}, f32[1,48,8,128]{3,1,2,0:T(8,128)S(1)}, u32[]{:S(2)}, u32[]{:S(2)}) collective-permute-start(f32[1,48,8,128]{3,1,2,0:T(8,128)S(1)} %maximum_bitcast_fusion), channel_id=1, source_target_pairs={{8,0},{16,8},{24,16},{9,1},{17,9},{25,17},{10,2},{18,10},{26,18},{... | collective-permute-start | bytes 589832 | tf_op jit(solution)/shard_map/ppermute | solution.py:30
  7.2 0.7 %subtract_add_fusion.1 = (s32[64,2]{0,1:T(2,128)S(1)}, s32[64,2]{0,1:T(2,128)S(1)}, s32[64,2]{0,1:T(2,128)S(1)}) fusion(s32[]{:T(128)S(6)} %mul.56, s32[]{:T(128)S(6)} %axis_index.23, s32[64,2]{0,1:T(2,128)} %param.11), kind=kLoop, calls=%fused_computation.17 | loop fusion | flops 2304 | bytes 2056 | tf_op jit(solution)/shard_map/add | solution.py:162
  8.0 1.9 %collective-permute-done = f32[1,48,8,128]{3,1,2,0:T(8,128)S(1)} collective-permute-done((f32[1,48,8,128]{3,1,2,0:T(8,128)S(1)}, f32[1,48,8,128]{3,1,2,0:T(8,128)S(1)}, u32[]{:S(2)}, u32[]{:S(2)}) %collective-permute-start) | collective-permute-done | bytes 196640 | tf_op jit(solution)/shard_map/ppermute | solution.py:27
  9.9 3.2 %collective-permute-done.1 = f32[1,48,8,128]{3,1,2,0:T(8,128)S(1)} collective-permute-done((f32[1,48,8,128]{3,1,2,0:T(8,128)S(1)}, f32[1,48,8,128]{3,1,2,0:T(8,128)S(1)}, u32[]{:S(2)}, u32[]{:S(2)}) %collective-permute-start.1) | collective-permute-done | bytes 196640 | tf_op jit(solution)/shard_map/ppermute | solution.py:30
  13.1 1.9 %collective-permute-start.2 = (f32[3,1,8,128]{3,1,2,0:T(1,128)S(1)}, f32[3,1,8,128]{3,1,2,0:T(1,128)S(1)}, u32[]{:S(2)}, u32[]{:S(2)}) collective-permute-start(f32[3,1,8,128]{3,1,2,0:T(1,128)S(1)} %get-tuple-element.35), channel_id=1, source_target_pairs={{0,1},{1,2},{2,3},{3,4},{4,5},{5,6},{6,7},{8,9},{9,10},{10,11},{11... | collective-permute-start | bytes 36872 | tf_op jit(solution)/shard_map/ppermute | solution.py:27
  15.1 4.5 %collective-permute-start.3 = (f32[3,1,8,128]{3,1,2,0:T(1,128)S(1)}, f32[3,1,8,128]{3,1,2,0:T(1,128)S(1)}, u32[]{:S(2)}, u32[]{:S(2)}) collective-permute-start(f32[3,1,8,128]{3,1,2,0:T(1,128)S(1)} %get-tuple-element.36), channel_id=1, source_target_pairs={{1,0},{2,1},{3,2},{4,3},{5,4},{6,5},{7,6},{9,8},{10,9},{11,10},{12... | collective-permute-start | bytes 36872 | tf_op jit(solution)/shard_map/ppermute | solution.py:30
  19.6 0.6 pad_add_fusion.refs_0_
  20.2 0.0 collective-permute-done.2
  20.2 0.8 %collective-permute-done.3 = f32[3,1,8,128]{3,1,2,0:T(1,128)S(1)} collective-permute-done((f32[3,1,8,128]{3,1,2,0:T(1,128)S(1)}, f32[3,1,8,128]{3,1,2,0:T(1,128)S(1)}, u32[]{:S(2)}, u32[]{:S(2)}) %collective-permute-start.3) | collective-permute-done | bytes 12320 | tf_op jit(solution)/shard_map/ppermute | solution.py:30
  21.0 0.1 pad_maximum_fusion
  21.1 0.9 %copy.6 = f32[3,50,8,128]{3,2,1,0:T(8,128)} copy(f32[3,50,8,128]{3,1,2,0:T(8,128)S(1)} %pad_maximum_fusion) | data formatting | bytes 1228800 | tf_op jit(solution)/shard_map/concatenate | solution.py:31
  22.0 24.9 %shard_map.55 = f32[150,8,128]{2,1,0:T(8,128)} custom-call(s32[4,64]{1,0:T(4,128)} %pad_add_fusion.refs_0_, f32[150,8,128]{2,1,0:T(8,128)} %bitcast.21, s32[64,128,128]{2,1,0:T(8,128)} %refs_2_.1), custom_call_target="tpu_custom_call" | custom-call | tf_op jit(solution)/shard_map/pallas_call | solution.py:122
  46.9 1.1 %fusion.3 = (f32[50,3,128]{2,1,0:T(4,128)S(1)}, f32[50,3,128]{2,1,0:T(4,128)S(1)}) fusion(f32[150,8,128]{2,1,0:T(8,128)} %shard_map.55), kind=kLoop, calls=%fused_computation.25 | loop fusion | bytes 307200 | tf_op jit(solution)/shard_map/slice | solution.py:173
  48.0 2.4 %collective-permute-start.4 = (f32[50,3,128]{2,1,0:T(4,128)S(1)}, f32[50,3,128]{2,1,0:T(4,128)S(1)}, u32[]{:S(2)}, u32[]{:S(2)}) collective-permute-start(f32[50,3,128]{2,1,0:T(4,128)S(1)} %get-tuple-element.34), channel_id=1, source_target_pairs={{8,0},{16,8},{24,16},{9,1},{17,9},{25,17},{10,2},{18,10},{26,18},{... | collective-permute-start | bytes 230408 | tf_op jit(solution)/shard_map/ppermute | solution.py:19
  50.3 3.5 %collective-permute-start.5 = (f32[50,3,128]{2,1,0:T(4,128)S(1)}, f32[50,3,128]{2,1,0:T(4,128)S(1)}, u32[]{:S(2)}, u32[]{:S(2)}) collective-permute-start(f32[50,3,128]{2,1,0:T(4,128)S(1)} %get-tuple-element.33), channel_id=1, source_target_pairs={{0,8},{8,16},{16,24},{1,9},{9,17},{17,25},{2,10},{10,18},{18,26},{... | collective-permute-start | bytes 230408 | tf_op jit(solution)/shard_map/ppermute | solution.py:19
  53.8 1.5 %collective-permute-done.4 = f32[50,3,128]{2,1,0:T(4,128)S(1)} collective-permute-done((f32[50,3,128]{2,1,0:T(4,128)S(1)}, f32[50,3,128]{2,1,0:T(4,128)S(1)}, u32[]{:S(2)}, u32[]{:S(2)}) %collective-permute-start.4) | collective-permute-done | bytes 76832 | tf_op jit(solution)/shard_map/ppermute | solution.py:19
  55.3 2.1 %collective-permute-done.5 = f32[50,3,128]{2,1,0:T(4,128)S(1)} collective-permute-done((f32[50,3,128]{2,1,0:T(4,128)S(1)}, f32[50,3,128]{2,1,0:T(4,128)S(1)}, u32[]{:S(2)}, u32[]{:S(2)}) %collective-permute-start.5) | collective-permute-done | bytes 76832 | tf_op jit(solution)/shard_map/ppermute | solution.py:19
  57.4 1.0 %slice_add_fusion = f32[50,3,128]{2,1,0:T(4,128)S(1)} fusion(f32[150,8,128]{2,1,0:T(8,128)} %shard_map.55, f32[50,3,128]{2,1,0:T(4,128)S(1)} %collective-permute-done.4, f32[50,3,128]{2,1,0:T(4,128)S(1)} %collective-permute-done.5), kind=kLoop, calls=%fused_computation.2 | loop fusion | flops 38400 | bytes 307200 | tf_op jit(solution)/shard_map/add | solution.py:173
  58.4 2.6 %collective-permute-start.6 = (f32[3,128]{1,0:T(4,128)S(1)}, f32[3,128]{1,0:T(4,128)S(1)}, u32[]{:S(2)}, u32[]{:S(2)}) collective-permute-start(f32[3,128]{1,0:T(4,128)S(1)} %get-tuple-element.38), channel_id=1, source_target_pairs={{1,0},{2,1},{3,2},{4,3},{5,4},{6,5},{7,6},{9,8},{10,9},{11,10},{12... | collective-permute-start | bytes 4616 | tf_op jit(solution)/shard_map/ppermute | solution.py:19
  61.0 1.9 %collective-permute-start.7 = (f32[3,128]{1,0:T(4,128)S(1)}, f32[3,128]{1,0:T(4,128)S(1)}, u32[]{:S(2)}, u32[]{:S(2)}) collective-permute-start(f32[3,128]{1,0:T(4,128)S(1)} %get-tuple-element.37), channel_id=1, source_target_pairs={{0,1},{1,2},{2,3},{3,4},{4,5},{5,6},{6,7},{8,9},{9,10},{10,11},{11... | collective-permute-start | bytes 4616 | tf_op jit(solution)/shard_map/ppermute | solution.py:19
  62.9 0.0 collective-permute-done.6
  63.0 3.9 %collective-permute-done.7 = f32[3,128]{1,0:T(4,128)S(1)} collective-permute-done((f32[3,128]{1,0:T(4,128)S(1)}, f32[3,128]{1,0:T(4,128)S(1)}, u32[]{:S(2)}, u32[]{:S(2)}) %collective-permute-start.7) | collective-permute-done | bytes 1568 | tf_op jit(solution)/shard_map/ppermute | solution.py:19
  66.8 0.6 copy.7
  (10 shorter events, 0.1 us)
Async XLA Ops:
  1.4 8.5 %collective-permute-start = (f32[1,48,8,128]{3,1,2,0:T(8,128)S(1)}, f32[1,48,8,128]{3,1,2,0:T(8,128)S(1)}, u32[]{:S(2)}, u32[]{:S(2)}) collective-permute-start(f32[1,48,8,128]{3,1,2,0:T(8,128)S(1)} %maximum_bitcast_fusion), channel_id=1, source_target_pairs={{0,8},{8,16},{16,24},{1,9},{9,17},{17,25},{2,10},{10,18},{18,26},{... | collective-permute-start | bytes 589832 | tf_op jit(solution)/shard_map/ppermute | solution.py:27
  4.9 8.3 %collective-permute-start.1 = (f32[1,48,8,128]{3,1,2,0:T(8,128)S(1)}, f32[1,48,8,128]{3,1,2,0:T(8,128)S(1)}, u32[]{:S(2)}, u32[]{:S(2)}) collective-permute-start(f32[1,48,8,128]{3,1,2,0:T(8,128)S(1)} %maximum_bitcast_fusion), channel_id=1, source_target_pairs={{8,0},{16,8},{24,16},{9,1},{17,9},{25,17},{10,2},{18,10},{26,18},{... | collective-permute-start | bytes 589832 | tf_op jit(solution)/shard_map/ppermute | solution.py:30
  13.1 7.1 %collective-permute-start.2 = (f32[3,1,8,128]{3,1,2,0:T(1,128)S(1)}, f32[3,1,8,128]{3,1,2,0:T(1,128)S(1)}, u32[]{:S(2)}, u32[]{:S(2)}) collective-permute-start(f32[3,1,8,128]{3,1,2,0:T(1,128)S(1)} %get-tuple-element.35), channel_id=1, source_target_pairs={{0,1},{1,2},{2,3},{3,4},{4,5},{5,6},{6,7},{8,9},{9,10},{10,11},{11... | collective-permute-start | bytes 36872 | tf_op jit(solution)/shard_map/ppermute | solution.py:27
  15.1 5.9 %collective-permute-start.3 = (f32[3,1,8,128]{3,1,2,0:T(1,128)S(1)}, f32[3,1,8,128]{3,1,2,0:T(1,128)S(1)}, u32[]{:S(2)}, u32[]{:S(2)}) collective-permute-start(f32[3,1,8,128]{3,1,2,0:T(1,128)S(1)} %get-tuple-element.36), channel_id=1, source_target_pairs={{1,0},{2,1},{3,2},{4,3},{5,4},{6,5},{7,6},{9,8},{10,9},{11,10},{12... | collective-permute-start | bytes 36872 | tf_op jit(solution)/shard_map/ppermute | solution.py:30
  48.0 7.4 %collective-permute-start.4 = (f32[50,3,128]{2,1,0:T(4,128)S(1)}, f32[50,3,128]{2,1,0:T(4,128)S(1)}, u32[]{:S(2)}, u32[]{:S(2)}) collective-permute-start(f32[50,3,128]{2,1,0:T(4,128)S(1)} %get-tuple-element.34), channel_id=1, source_target_pairs={{8,0},{16,8},{24,16},{9,1},{17,9},{25,17},{10,2},{18,10},{26,18},{... | collective-permute-start | bytes 230408 | tf_op jit(solution)/shard_map/ppermute | solution.py:19
  50.3 7.1 %collective-permute-start.5 = (f32[50,3,128]{2,1,0:T(4,128)S(1)}, f32[50,3,128]{2,1,0:T(4,128)S(1)}, u32[]{:S(2)}, u32[]{:S(2)}) collective-permute-start(f32[50,3,128]{2,1,0:T(4,128)S(1)} %get-tuple-element.33), channel_id=1, source_target_pairs={{0,8},{8,16},{16,24},{1,9},{9,17},{17,25},{2,10},{10,18},{18,26},{... | collective-permute-start | bytes 230408 | tf_op jit(solution)/shard_map/ppermute | solution.py:19
  58.4 4.5 %collective-permute-start.6 = (f32[3,128]{1,0:T(4,128)S(1)}, f32[3,128]{1,0:T(4,128)S(1)}, u32[]{:S(2)}, u32[]{:S(2)}) collective-permute-start(f32[3,128]{1,0:T(4,128)S(1)} %get-tuple-element.38), channel_id=1, source_target_pairs={{1,0},{2,1},{3,2},{4,3},{5,4},{6,5},{7,6},{9,8},{10,9},{11,10},{12... | collective-permute-start | bytes 4616 | tf_op jit(solution)/shard_map/ppermute | solution.py:19
  61.0 5.8 %collective-permute-start.7 = (f32[3,128]{1,0:T(4,128)S(1)}, f32[3,128]{1,0:T(4,128)S(1)}, u32[]{:S(2)}, u32[]{:S(2)}) collective-permute-start(f32[3,128]{1,0:T(4,128)S(1)} %get-tuple-element.37), channel_id=1, source_target_pairs={{0,1},{1,2},{2,3},{3,4},{4,5},{5,6},{6,7},{8,9},{9,10},{10,11},{11... | collective-permute-start | bytes 4616 | tf_op jit(solution)/shard_map/ppermute | solution.py:19

commit v2 on v1

v2 whole, which is shorter than its diff:
```python
import math

import jax
import jax.numpy as jnp
from jax import lax
from jax.experimental import pallas as pl
from jax.experimental.pallas import tpu as pltpu
from jax.sharding import PartitionSpec as P

horizon = 3.0
stiffness = 2.0
onset_stretch = 0.02
final_stretch = 0.05

MESH = pl.DeviceIdType.MESH
STRIPS = (0, -1, 1)
DIRECTIONS = tuple((es, et) for es in (-1, 1, 0) for et in (0, -1, 1) if (es, et) != (0, 0))
EDGE = 8


def whole_rows(per, es):
    return pl.ds(STRIPS.index(es) * per, per)


def edge_rows(per, es, et):
    return pl.ds(3 * per + (2 * STRIPS.index(es) + (et > 0)) * EDGE, EDGE)


def split_rows(rows):
    row = lax.broadcasted_iota(jnp.int32, rows.shape, 0)
    lead = jnp.where(row < 3, rows, jnp.where(row == 3, 1.0, 0.0))
    high = lead.astype(jnp.bfloat16).astype(jnp.float32)
    return jnp.concatenate([high, lead - high], axis=0).astype(jnp.bfloat16)


def pair_pull(first, second, bonds):
    def norm2(c):
        x, y, z = (second[c + i] - first(c + i) for i in range(3))
        return x * x + y * y + z * z

    now2, ref2 = norm2(0), norm2(3)
    inv_now, inv_ref = lax.rsqrt(now2), lax.rsqrt(ref2)
    ratio = now2 * inv_now * inv_ref
    influence = jnp.maximum(0.0, stiffness - ref2 * inv_ref * (stiffness / horizon))
    span = final_stretch - onset_stretch
    soften = jnp.clip((1.0 + final_stretch) / span - ratio * (1.0 / span), 0.0, 1.0)
    pull = (ratio - 1.0) * influence * (soften * inv_now)
    return jnp.where(bonds != 0, pull, 0.0)


def dot_rows(rows, matrix):
    return lax.dot_general(rows, matrix, (((1,), (0,)), ((), ())), preferred_element_type=jnp.float32)


def dot_columns(rows, matrix):
    return lax.dot_general(rows, matrix, (((1,), (1,)), ((), ())), preferred_element_type=jnp.float32)


def force_kernel(
    scalars_ref, ends_ref, coords_ref, displacement_ref, bonds_hbm, out_ref,
    table, owned, spread, bonds, gains, forces, from_strip, from_edge,
    load_sem, send_sem, recv_sem, back_sem, home_sem,
):
    per, points = coords_ref.shape[0], coords_ref.shape[2]
    pair_count = bonds.shape[0]
    groups = load_sem.shape[0]
    group = pair_count // groups
    strip, tile = lax.axis_index("strip"), lax.axis_index("tile")
    strips, tiles = lax.axis_size("strip"), lax.axis_size("tile")

    def load(g):
        part = pl.ds(g * group, group)
        return pltpu.make_async_copy(bonds_hbm.at[part], bonds.at[part], load_sem.at[g])

    for g in range(groups):
        load(g).start()

    def exists(es, et):
        s, t = strip + es, tile + et
        return (s >= 0) & (s < strips) & (t >= 0) & (t < tiles)

    barrier = pltpu.get_barrier_semaphore()
    for es, et in DIRECTIONS:
        @pl.when(exists(es, et))
        def _(es=es, et=et):
            pl.semaphore_signal(
                barrier, inc=1, device_id=(strip + es, tile + et), device_id_type=MESH
            )

    place = lax.broadcasted_iota(jnp.int32, (per, points), 0) + tile * per
    for c in range(3):
        local = coords_ref[:, c, :]
        base = (4 * strip).astype(jnp.float32) if c == 0 else (
            4.0 * place.astype(jnp.float32) if c == 1 else 0.0)
        local = local - base - (3.5 if c == 2 else 1.5)
        table[3 + c, 0:per, :] = local
        table[c, 0:per, :] = local + displacement_ref[:, c, :]

    near = sum(
        jnp.where(exists(es, et), 1, 0) for es, et in DIRECTIONS
    )
    pl.semaphore_wait(barrier, near)

    def halo(i):
        es, et = DIRECTIONS[i]
        if et == 0:
            source, target = pl.ds(0, per), whole_rows(per, -es)
        else:
            source = pl.ds(per - EDGE if et > 0 else 0, EDGE)
            target = edge_rows(per, -es, -et)
        return pltpu.make_async_remote_copy(
            src_ref=table.at[:, source],
            dst_ref=table.at[:, target],
            send_sem=send_sem.at[i],
            recv_sem=recv_sem.at[i],
            device_id=(strip + es, tile + et),
            device_id_type=MESH,
        )

    def back(i):
        es, et = DIRECTIONS[i]
        if et == 0:
            source, target = whole_rows(per, es), from_strip.at[0 if es < 0 else 1]
        else:
            source, target = edge_rows(per, es, et), from_edge.at[i]
        return pltpu.make_async_remote_copy(
            src_ref=forces.at[:, source],
            dst_ref=target,
            send_sem=back_sem.at[i],
            recv_sem=home_sem.at[i],
            device_id=(strip + es, tile + et),
            device_id_type=MESH,
        )

    def each(step, opposite):
        for i, (es, et) in enumerate(DIRECTIONS):
            here = exists(-es, -et) if opposite else exists(es, et)
            pl.when(here)(lambda i=i: step(i))

    each(lambda i: halo(i).start(), False)

    def widen(a, carry):
        rows = [table[c, pl.ds(a, 1), :] for c in range(6)]
        row = lax.broadcasted_iota(jnp.int32, (8, points), 0)
        tall = jnp.zeros((8, points), jnp.float32)
        for c in range(6):
            tall = jnp.where(row == c, rows[c], tall)
        owned[a] = tall
        columns = tall.T
        for c in range(6):
            spread[a, c] = jnp.broadcast_to(columns[:, c : c + 1], (points, points))
        return carry

    lax.fori_loop(0, per, widen, 0, unroll=2)

    each(lambda i: halo(i).wait_recv(), True)

    chunk = math.gcd(points, 32)
    row = lax.broadcasted_iota(jnp.int32, (8, points), 0)

    def visit(k, carry):
        first, second = scalars_ref[0, k], scalars_ref[1, k]
        move_x = scalars_ref[2, k].astype(jnp.float32)
        move_y = scalars_ref[3, k].astype(jnp.float32)
        second_flat = [table[c, pl.ds(second, 1), :] for c in range(6)]
        moved = [
            second_flat[0] + move_x, second_flat[1] + move_y, second_flat[2],
            second_flat[3] + move_x, second_flat[4] + move_y, second_flat[5],
        ]
        leads, rests = [], []
        for at in range(0, points, chunk):
            pull = pair_pull(
                lambda c: spread[first, c, at : at + chunk, :], moved, bonds[k, at : at + chunk]
            )
            lead = pull.astype(jnp.bfloat16)
            leads.append(lead)
            rests.append((pull - lead.astype(jnp.float32)).astype(jnp.bfloat16))
        lead, rest = jnp.concatenate(leads, axis=0), jnp.concatenate(rests, axis=0)
        first_rows = owned[first]
        second_rows = jnp.where(
            row == 0, second_flat[0], jnp.where(row == 1, second_flat[1], second_flat[2])
        )
        first_split, second_split = split_rows(first_rows), split_rows(second_rows)
        to_first = dot_columns(second_split, lead) + dot_columns(second_split, rest)
        to_second = dot_rows(first_split, lead) + dot_rows(first_split, rest)
        to_first = to_first[:8] + to_first[8:]
        to_second = to_second[:8] + to_second[8:]
        move = jnp.where(row == 0, move_x, jnp.where(row == 1, move_y, 0.0))
        to_first = to_first - (first_rows - move) * to_first[3:4]
        to_second = to_second - (second_rows + move) * to_second[3:4]
        for c in range(3):
            gains[c, pl.ds(k, 1), :] = to_first[c : c + 1]
            gains[c, pl.ds(pair_count + k, 1), :] = to_second[c : c + 1]
        return carry

    def visit_group(g, carry):
        load(g).wait()
        return lax.fori_loop(0, group, lambda i, c: visit(g * group + i, c), carry, unroll=2)

    lax.fori_loop(0, groups, visit_group, 0)

    pieces = []
    for c in range(3):
        value = gains[c]
        for unused in range(3):
            piece = value.astype(jnp.bfloat16)
            pieces.append(piece)
            value = value - piece.astype(jnp.float32)
    pieces = jnp.concatenate(pieces, axis=1)

    def gather(start, count):
        slot = lax.broadcasted_iota(jnp.int32, (count, 2 * pair_count), 0) + start
        weight = jnp.where(slot == ends_ref[0:1, :], 1.0, 0.0).astype(jnp.bfloat16)
        sums = dot_rows(weight, pieces)
        for c in range(3):
            parts = [sums[:, (3 * c + j) * points : (3 * c + j + 1) * points] for j in range(3)]
            forces[c, start : start + count, :] = parts[0] + (parts[1] + parts[2])

    gather(per, forces.shape[1] - per)
    each(lambda i: back(i).start(), False)
    gather(0, per)

    def receive(i):
        es, et = DIRECTIONS[i]
        back(i).wait_recv()
        if et == 0:
            forces[:, 0:per, :] += from_strip[0 if es < 0 else 1]
        else:
            at = per - EDGE if et < 0 else 0
            forces[:, at : at + EDGE, :] += from_edge[i]

    each(receive, True)
    out_ref[...] = forces[:, 0:per, :]
    each(lambda i: halo(i).wait_send(), False)
    each(lambda i: back(i).wait_send(), False)


def on_device(coords, displacement, pairs, intact):
    per, points = coords.shape[0], coords.shape[2]
    pair_count = pairs.shape[0]
    groups = math.gcd(pair_count, 8)
    strip_tiles = per * lax.axis_size("tile")
    strip_index = lax.axis_index("strip")
    tile_index = lax.axis_index("tile")
    flat = pairs.T
    strip_of, place_of = flat // strip_tiles, flat % strip_tiles
    beside = strip_of - strip_index
    order = jnp.where(beside == 0, 0, jnp.where(beside < 0, 1, 2))
    at = place_of - tile_index * per
    edge = 3 * per + 2 * EDGE * order
    slot = jnp.where(at < 0, edge + EDGE - 1, jnp.where(at >= per, edge + EDGE, order * per + at))
    scalars = jnp.concatenate(
        [slot, 4 * (strip_of[1:] - strip_of[:1]), 4 * (place_of[1:] - place_of[:1])], axis=0
    )
    ends = slot.reshape(1, 2 * pair_count)
    slots = 3 * per + 6 * EDGE
    many = len(DIRECTIONS)
    vmem = pl.BlockSpec(memory_space=pltpu.VMEM)
    forces = pl.pallas_call(
        force_kernel,
        in_specs=[
            pl.BlockSpec(memory_space=pltpu.SMEM), vmem, vmem, vmem,
            pl.BlockSpec(memory_space=pl.ANY),
        ],
        out_specs=vmem,
        out_shape=jax.ShapeDtypeStruct((3, per, points), jnp.float32),
        scratch_shapes=[
            pltpu.VMEM((6, slots, points), jnp.float32),
            pltpu.VMEM((per, 8, points), jnp.float32),
            pltpu.VMEM((per, 6, points, points), jnp.float32),
            pltpu.VMEM(intact.shape, jnp.int32),
            pltpu.VMEM((3, 2 * pair_count, points), jnp.float32),
            pltpu.VMEM((3, slots, points), jnp.float32),
            pltpu.VMEM((2, 3, per, points), jnp.float32),
            pltpu.VMEM((many, 3, EDGE, points), jnp.float32),
            pltpu.SemaphoreType.DMA((groups,)),
            pltpu.SemaphoreType.DMA((many,)),
            pltpu.SemaphoreType.DMA((many,)),
            pltpu.SemaphoreType.DMA((many,)),
            pltpu.SemaphoreType.DMA((many,)),
        ],
        compiler_params=pltpu.CompilerParams(collective_id=0, has_side_effects=True),
    )(scalars, ends, coords, displacement, intact)
    return jnp.transpose(forces, (1, 0, 2))


def solution(mesh):
    placed = (
        P(("strip", "tile"), None, None),
        P(("strip", "tile"), None, None),
        P(("strip", "tile"), None),
        P(("strip", "tile"), None, None),
    )
    return jax.shard_map(
        on_device,
        mesh=mesh,
        in_specs=placed,
        out_specs=P(("strip", "tile"), None, None),
        check_vma=False,
    )
```

time: 67.9 us -> 36.5 us (0.54)
  starting transfers between devices: 22.6 us -> 0 us
  waiting for transfers between devices: 13.4 us -> 0 us
  Pallas kernels: 24.9 us -> 29.3 us
  local copies, waits for them, and re-layouts: 2.81 us -> 5.29 us
  other arithmetic: 3.58 us -> 1.29 us
    ppermute x8 -> x0, starting transfers between devices: 22.6 us -> none  [the longest x4 10.3 us: from_behind(): lax.ppermute(value, axis, [(source, source + steps) for source in range(f...]
    ppermute x8 -> x0, waiting for transfers between devices: 13.4 us -> none  [the longest x4 7.45 us: from_behind(): lax.ppermute(value, axis, [(source, source + steps) for source in range(f...]
    unnamed x0 -> x3, local copies, waits for them, and re-layouts: none -> 4.62 us
    pallas_call x1, Pallas kernels: 24.9 us -> 29.3 us  [on_device(): pl.pallas_call(force_kernel, in_specs=[pl.BlockSpec(memory_space=pltpu.SM...]
    add x3 -> x0, other arithmetic: 2.71 us -> none  [the longest x1 1.03 us: on_device(): now = local + displacement]
    slice x2 -> x0, local copies, waits for them, and re-layouts: 1.07 us -> none  [the longest x1 1.06 us: on_device(): strip_row = buffer[1] + strip_pass(buffer[0], buffer[2])]
    concatenate x2 -> x0, local copies, waits for them, and re-layouts: 1.01 us -> none  [the longest x1 0.93 us: padded(): block = jnp.concatenate([low, block, high], axis=dim)]
    select_n x0 -> x1, other arithmetic: none -> 0.7 us  [on_device(): jnp.where(at < 0, edge + EDGE - 1, jnp.where(at >= per, edge + EDGE, orde...]
  transfers between devices with their start and end apart: 8 -> 0, of which waited for: 6 -> 0; matrix products, arithmetic and copies ran while one was open for 2% -> 0% of each run, Pallas kernels for 0% -> 0%
where the time goes in v2:
time: 36.5 us; the launch traced here: 35.9 us
  Pallas kernels  29.3 us (80%)
  local copies, waits for them, and re-layouts  5.29 us (14%)
  other arithmetic  1.29 us (4%)
    pallas_call x1, Pallas kernels, on_device(): pl.pallas_call(force_kernel, in_specs=[pl.BlockSpec(memory_space=pltpu.SM...  29.3 us
    unnamed x3, local copies, waits for them, and re-layouts  4.62 us

profile of v2, /device:TPU:12, one launch (start us, length us, event | category | flops | bytes accessed | tf_op | source)
XLA Modules:
  0.0 35.9 jit_solution(17755682804029397648)
XLA Ops:
  0.0 0.7 %compare_select_fusion.3 = (s32[2,64]{1,0:T(2,128)S(1)}, s32[2,64]{1,0:T(2,128)S(1)}, s32[2,64]{1,0:T(2,128)S(1)}) fusion(s32[]{:T(128)S(6)} %axis_index.25, s32[]{:T(128)S(6)} %mul.18, s32[64,2]{0,1:T(2,128)} %param.6), kind=kLoop, calls=%fused_computation.6 | loop fusion | flops 3456 | bytes 2056 | tf_op jit(solution)/shard_map/jit(_where)/select_n | solution.py:251
  0.7 0.7 %reshape.3.ends_ref = s32[1,128]{1,0:T(1,128)} reshape(s32[2,64]{1,0:T(2,128)S(1)} %get-tuple-element.5) | data formatting | bytes 1024 | tf_op jit(solution)/shard_map/reshape | solution.py:255
  1.4 0.6 %pad_add_fusion.scalars_ref = s32[4,64]{1,0:T(4,128)} fusion(s32[1,64]{1,0:T(1,128)S(1)} %get-tuple-element.8, s32[1,64]{1,0:T(1,128)S(1)} %get-tuple-element.9, s32[2,64]{1,0:T(2,128)S(1)} %get-tuple-element.5), kind=kLoop, calls=%fused_computation | loop fusion | flops 512 | bytes 2048 | tf_op jit(solution)/shard_map/concatenate | solution.py:252
  2.0 1.5 %copy.5.coords_ref = f32[48,3,128]{2,1,0:T(4,128)} copy(f32[48,3,128]{2,0,1:T(8,128)} %param.4) | data formatting | bytes 147456 | tf_op args[0]
  3.5 1.6 %copy.6.displacement_ref = f32[48,3,128]{2,1,0:T(4,128)} copy(f32[48,3,128]{2,0,1:T(8,128)} %param.5) | data formatting | bytes 147456 | tf_op args[1]
  5.1 29.3 %shard_map.46 = f32[3,48,128]{2,1,0:T(8,128)} custom-call(s32[4,64]{1,0:T(4,128)} %pad_add_fusion.scalars_ref, s32[1,128]{1,0:T(1,128)} %reshape.3.ends_ref, f32[48,3,128]{2,1,0:T(4,128)} %copy.5.coords_ref, f32[48,3,128]{2,1,0:T(4,128)} %copy.6.displacement_ref, s32[64,128,128]{2,1,0:T(8,128)} %bonds_hbm.1), custom_call_target="tpu_custom_call" | custom-call | tf_op jit(solution)/shard_map/pallas_call | solution.py:259
  34.4 1.5 %copy.8 = f32[48,3,128]{2,0,1:T(8,128)} copy(f32[48,3,128]{2,0,1:T(8,128)} %bitcast.19) | data formatting | bytes 147456
  (1 shorter events, 0.0 us)

commit v3 on v2

--- a/solution.py
+++ b/solution.py
@@ -61,7 +61,7 @@
     table, owned, spread, bonds, gains, forces, from_strip, from_edge,
     load_sem, send_sem, recv_sem, back_sem, home_sem,
 ):
-    per, points = coords_ref.shape[0], coords_ref.shape[2]
+    per, points = coords_ref.shape[1], coords_ref.shape[2]
     pair_count = bonds.shape[0]
     groups = load_sem.shape[0]
     group = pair_count // groups
@@ -89,12 +89,17 @@
 
     place = lax.broadcasted_iota(jnp.int32, (per, points), 0) + tile * per
     for c in range(3):
-        local = coords_ref[:, c, :]
+        local = coords_ref[c]
         base = (4 * strip).astype(jnp.float32) if c == 0 else (
             4.0 * place.astype(jnp.float32) if c == 1 else 0.0)
         local = local - base - (3.5 if c == 2 else 1.5)
+        now = local + displacement_ref[c]
         table[3 + c, 0:per, :] = local
-        table[c, 0:per, :] = local + displacement_ref[:, c, :]
+        table[c, 0:per, :] = now
+        owned[:, 3 + c, :] = local
+        owned[:, c, :] = now
+    for c in (6, 7):
+        owned[:, c, :] = jnp.zeros((per, points), jnp.float32)
 
     near = sum(
         jnp.where(exists(es, et), 1, 0) for es, et in DIRECTIONS
@@ -139,19 +144,15 @@
 
     each(lambda i: halo(i).start(), False)
 
-    def widen(a, carry):
-        rows = [table[c, pl.ds(a, 1), :] for c in range(6)]
-        row = lax.broadcasted_iota(jnp.int32, (8, points), 0)
-        tall = jnp.zeros((8, points), jnp.float32)
-        for c in range(6):
-            tall = jnp.where(row == c, rows[c], tall)
-        owned[a] = tall
-        columns = tall.T
-        for c in range(6):
-            spread[a, c] = jnp.broadcast_to(columns[:, c : c + 1], (points, points))
+    def widen(g, carry):
+        columns = owned[pl.ds(g * (points // 8), points // 8)].reshape(points, points).T
+        for j in range(points // 8):
+            for c in range(6):
+                column = columns[:, 8 * j + c : 8 * j + c + 1]
+                spread[g * (points // 8) + j, c] = jnp.broadcast_to(column, (points, points))
         return carry
 
-    lax.fori_loop(0, per, widen, 0, unroll=2)
+    lax.fori_loop(0, per * 8 // points, widen, 0)
 
     each(lambda i: halo(i).wait_recv(), True)
 
@@ -199,26 +200,33 @@
 
     lax.fori_loop(0, groups, visit_group, 0)
 
-    pieces = []
-    for c in range(3):
-        value = gains[c]
-        for unused in range(3):
-            piece = value.astype(jnp.bfloat16)
-            pieces.append(piece)
-            value = value - piece.astype(jnp.float32)
-    pieces = jnp.concatenate(pieces, axis=1)
-
-    def gather(start, count):
-        slot = lax.broadcasted_iota(jnp.int32, (count, 2 * pair_count), 0) + start
-        weight = jnp.where(slot == ends_ref[0:1, :], 1.0, 0.0).astype(jnp.bfloat16)
+    def pieces_of(start):
+        pieces = []
+        for c in range(3):
+            value = gains[c, start : start + pair_count]
+            for unused in range(3):
+                piece = value.astype(jnp.bfloat16)
+                pieces.append(piece)
+                value = value - piece.astype(jnp.float32)
+        return jnp.concatenate(pieces, axis=1)
+
+    ends = ends_ref[...]
+    second_pieces = pieces_of(pair_count)
+
+    def gather(start, count, which, pieces):
+        slot = lax.broadcasted_iota(jnp.int32, (count, pair_count), 0) + start
+        weight = jnp.where(slot == ends[which : which + 1], 1.0, 0.0).astype(jnp.bfloat16)
         sums = dot_rows(weight, pieces)
         for c in range(3):
             parts = [sums[:, (3 * c + j) * points : (3 * c + j + 1) * points] for j in range(3)]
-            forces[c, start : start + count, :] = parts[0] + (parts[1] + parts[2])
-
-    gather(per, forces.shape[1] - per)
+            yield parts[0] + (parts[1] + parts[2])
+
+    for c, total in enumerate(gather(per, forces.shape[1] - per, 1, second_pieces)):
+        forces[c, per:, :] = total
     each(lambda i: back(i).start(), False)
-    gather(0, per)
+    both = zip(gather(0, per, 1, second_pieces), gather(0, per, 0, pieces_of(0)))
+    for c, (second_total, first_total) in enumerate(both):
+        forces[c, 0:per, :] = second_total + first_total
 
     def receive(i):
         es, et = DIRECTIONS[i]
@@ -249,10 +257,9 @@
     at = place_of - tile_index * per
     edge = 3 * per + 2 * EDGE * order
     slot = jnp.where(at < 0, edge + EDGE - 1, jnp.where(at >= per, edge + EDGE, order * per + at))
-    scalars = jnp.concatenate(
+    listed = jnp.concatenate(
         [slot, 4 * (strip_of[1:] - strip_of[:1]), 4 * (place_of[1:] - place_of[:1])], axis=0
     )
-    ends = slot.reshape(1, 2 * pair_count)
     slots = 3 * per + 6 * EDGE
     many = len(DIRECTIONS)
     vmem = pl.BlockSpec(memory_space=pltpu.VMEM)
@@ -280,7 +287,7 @@
             pltpu.SemaphoreType.DMA((many,)),
         ],
         compiler_params=pltpu.CompilerParams(collective_id=0, has_side_effects=True),
-    )(scalars, ends, coords, displacement, intact)
+    )(listed, listed, coords.transpose(1, 0, 2), displacement.transpose(1, 0, 2), intact)
     return jnp.transpose(forces, (1, 0, 2))
 
 

time: 36.5 us -> 31.2 us (0.85)
  the two profiles are of different devices: /device:TPU:12 before, /device:TPU:1 now
where the time goes in v3:
time: 31.2 us; the launch traced here: 31 us
  Pallas kernels  28.1 us (90%)
  local copies, waits for them, and re-layouts  1.52 us (5%)
  other arithmetic  1.29 us (4%)
    pallas_call x1, Pallas kernels, on_device(): pl.pallas_call(force_kernel, in_specs=[pl.BlockSpec(memory_space=pltpu.SM...  28.1 us
    unnamed x1, local copies, waits for them, and re-layouts  1.52 us
    select_n x1, other arithmetic, on_device(): jnp.where(at < 0, edge + EDGE - 1, jnp.where(at >= per, edge + EDGE, orde...  0.7 us

profile of v3, /device:TPU:1, one launch (start us, length us, event | category | flops | bytes accessed | tf_op | source)
XLA Modules:
  0.0 31.0 jit_solution(7194327508363489752)
XLA Ops:
  0.0 0.7 %compare_select_fusion.3 = (s32[2,64]{1,0:T(2,128)S(1)}, s32[2,64]{1,0:T(2,128)S(1)}, s32[2,64]{1,0:T(2,128)S(1)}) fusion(s32[]{:T(128)S(6)} %axis_index.25, s32[]{:T(128)S(6)} %mul.18, s32[64,2]{0,1:T(2,128)} %param.6), kind=kLoop, calls=%fused_computation.6 | loop fusion | flops 3456 | bytes 2056 | tf_op jit(solution)/shard_map/jit(_where)/select_n | solution.py:259
  0.7 0.6 %pad_add_fusion.scalars_ref.ends_ref = s32[4,64]{1,0:T(4,128)} fusion(s32[1,64]{1,0:T(1,128)S(1)} %get-tuple-element.8, s32[1,64]{1,0:T(1,128)S(1)} %get-tuple-element.9, s32[2,64]{1,0:T(2,128)S(1)} %get-tuple-element.5), kind=kLoop, calls=%fused_computation | loop fusion | flops 512 | bytes 2048 | tf_op jit(solution)/shard_map/concatenate | solution.py:260
  1.3 28.1 %shard_map.46 = f32[3,48,128]{2,1,0:T(8,128)} custom-call(s32[4,64]{1,0:T(4,128)} %pad_add_fusion.scalars_ref.ends_ref, s32[4,64]{1,0:T(4,128)} %pad_add_fusion.scalars_ref.ends_ref, f32[3,48,128]{2,1,0:T(8,128)} %bitcast.22, f32[3,48,128]{2,1,0:T(8,128)} %bitcast.23, s32[64,128,128]{2,1,0:T(8,128)} %bonds_hbm.1), custom_call_target="tpu_custom_call" | custom-call | tf_op jit(solution)/shard_map/pallas_call | solution.py:266
  29.5 1.5 %copy.6 = f32[48,3,128]{2,0,1:T(8,128)} copy(f32[48,3,128]{2,0,1:T(8,128)} %bitcast.21) | data formatting | bytes 147456
  (1 shorter events, 0.0 us)

commit v4 on v3

--- a/solution.py
+++ b/solution.py
@@ -57,7 +57,7 @@
 
 
 def force_kernel(
-    scalars_ref, ends_ref, coords_ref, displacement_ref, bonds_hbm, out_ref,
+    scalars_ref, ends_ref, coords_ref, displacement_ref, bonds_hbm, out_ref, received_ref,
     table, owned, spread, bonds, gains, forces, from_strip, from_edge,
     load_sem, send_sem, recv_sem, back_sem, home_sem,
 ):
@@ -196,7 +196,7 @@
 
     def visit_group(g, carry):
         load(g).wait()
-        return lax.fori_loop(0, group, lambda i, c: visit(g * group + i, c), carry, unroll=2)
+        return lax.fori_loop(0, group, lambda i, c: visit(g * group + i, c), carry, unroll=group)
 
     lax.fori_loop(0, groups, visit_group, 0)
 
@@ -232,13 +232,14 @@
         es, et = DIRECTIONS[i]
         back(i).wait_recv()
         if et == 0:
-            forces[:, 0:per, :] += from_strip[0 if es < 0 else 1]
+            received_ref[...] += from_strip[0 if es < 0 else 1]
         else:
             at = per - EDGE if et < 0 else 0
-            forces[:, at : at + EDGE, :] += from_edge[i]
-
+            received_ref[:, at : at + EDGE, :] += from_edge[i]
+
+    out_ref[...] = forces[:, 0:per, :]
+    received_ref[...] = jnp.zeros_like(received_ref)
     each(receive, True)
-    out_ref[...] = forces[:, 0:per, :]
     each(lambda i: halo(i).wait_send(), False)
     each(lambda i: back(i).wait_send(), False)
 
@@ -250,27 +251,28 @@
     strip_tiles = per * lax.axis_size("tile")
     strip_index = lax.axis_index("strip")
     tile_index = lax.axis_index("tile")
-    flat = pairs.T
-    strip_of, place_of = flat // strip_tiles, flat % strip_tiles
-    beside = strip_of - strip_index
+    first, second = pairs.T[:1], pairs.T[1:]
+    row = lax.broadcasted_iota(jnp.int32, (4, pair_count), 0)
+    tiles = jnp.where(row == 0, first, second)
+    beside = tiles // strip_tiles - strip_index
     order = jnp.where(beside == 0, 0, jnp.where(beside < 0, 1, 2))
-    at = place_of - tile_index * per
+    at = tiles % strip_tiles - tile_index * per
     edge = 3 * per + 2 * EDGE * order
     slot = jnp.where(at < 0, edge + EDGE - 1, jnp.where(at >= per, edge + EDGE, order * per + at))
-    listed = jnp.concatenate(
-        [slot, 4 * (strip_of[1:] - strip_of[:1]), 4 * (place_of[1:] - place_of[:1])], axis=0
-    )
+    over = second // strip_tiles - first // strip_tiles
+    along = second % strip_tiles - first % strip_tiles
+    listed = jnp.where(row < 2, slot, 4 * jnp.where(row == 2, over, along))
     slots = 3 * per + 6 * EDGE
     many = len(DIRECTIONS)
     vmem = pl.BlockSpec(memory_space=pltpu.VMEM)
-    forces = pl.pallas_call(
+    own, received = pl.pallas_call(
         force_kernel,
         in_specs=[
             pl.BlockSpec(memory_space=pltpu.SMEM), vmem, vmem, vmem,
             pl.BlockSpec(memory_space=pl.ANY),
         ],
-        out_specs=vmem,
-        out_shape=jax.ShapeDtypeStruct((3, per, points), jnp.float32),
+        out_specs=(vmem, vmem),
+        out_shape=(jax.ShapeDtypeStruct((3, per, points), jnp.float32),) * 2,
         scratch_shapes=[
             pltpu.VMEM((6, slots, points), jnp.float32),
             pltpu.VMEM((per, 8, points), jnp.float32),
@@ -288,7 +290,7 @@
         ],
         compiler_params=pltpu.CompilerParams(collective_id=0, has_side_effects=True),
     )(listed, listed, coords.transpose(1, 0, 2), displacement.transpose(1, 0, 2), intact)
-    return jnp.transpose(forces, (1, 0, 2))
+    return jnp.transpose(own + received, (1, 0, 2))
 
 
 def solution(mesh):

time: 31.2 us -> 27.5 us (0.88)
  Pallas kernels: 28.1 us -> 24.2 us
  other arithmetic: 1.29 us -> 3.02 us
  local copies, waits for them, and re-layouts: 1.52 us -> 0 us
    pallas_call x1, Pallas kernels: 28.1 us -> 24.2 us  [on_device(): pl.pallas_call(force_kernel, in_specs=[pl.BlockSpec(memory_space=pltpu.SM...]
    transpose x0 -> x1, other arithmetic: none -> 1.56 us  [on_device(): return jnp.transpose(own + received, (1, 0, 2))]
    unnamed x1 -> x0, local copies, waits for them, and re-layouts: 1.52 us -> none
    broadcast_in_dim x0 -> x1, other arithmetic: none -> 0.77 us  [on_device(): tiles = jnp.where(row == 0, first, second)]
    concatenate x1 -> x0, other arithmetic: 0.59 us -> none  [on_device(): jnp.concatenate([slot, 4 * (strip_of[1:] - strip_of[:1]), 4 * (place_of[1...]
where the time goes in v4:
time: 27.5 us; the launch traced here: 27.3 us
  Pallas kernels  24.2 us (88%)
  other arithmetic  3.02 us (11%)
    pallas_call x1, Pallas kernels, on_device(): pl.pallas_call(force_kernel, in_specs=[pl.BlockSpec(memory_space=pltpu.SM...  24.2 us
    transpose x1, other arithmetic, on_device(): return jnp.transpose(own + received, (1, 0, 2))  1.56 us
    broadcast_in_dim x1, other arithmetic, on_device(): tiles = jnp.where(row == 0, first, second)  0.77 us
    select_n x1, other arithmetic, on_device(): listed = jnp.where(row < 2, slot, 4 * jnp.where(row == 2, over, along))  0.67 us

profile of v4, /device:TPU:1, one launch (start us, length us, event | category | flops | bytes accessed | tf_op | source)
XLA Modules:
  0.0 27.3 jit_solution(12414423843488185450)
XLA Ops:
  0.0 0.8 %slice_bitcast_fusion.1 = (s32[64]{0:T(128)S(1)}, s32[64]{0:T(128)S(1)}, s32[64]{0:T(128)S(1)}, s32[64]{0:T(128)S(1)}) fusion(s32[2,64]{1,0:T(2,128)} %bitcast.15), kind=kLoop, calls=%fused_computation.26 | loop fusion | flops 1664 | bytes 1536 | tf_op jit(solution)/shard_map/jit(_where)/broadcast_in_dim | solution.py:256
  0.8 0.7 %multiply_select_fusion.scalars_ref.ends_ref = s32[4,64]{1,0:T(4,128)} fusion(s32[64]{0:T(128)S(1)} %get-tuple-element.11, s32[64]{0:T(128)S(1)} %get-tuple-element.10, s32[]{:T(128)S(6)} %axis_index.25, s32[]{:T(128)S(6)} %mul.18, s32[64]{0:T(128)S(1)} %get-tuple-element.12, s32[64]{0:T(128)S(1)} %get-tuple-element.9, ...), kind=kLoop, calls=%fused_computation.12 | loop fusion | flops 7936 | bytes 2068 | tf_op jit(solution)/shard_map/jit(_where)/select_n | solution.py:264
  1.5 24.2 %shard_map.46 = (f32[3,48,128]{2,1,0:T(8,128)}, f32[3,48,128]{2,1,0:T(8,128)}) custom-call(s32[4,64]{1,0:T(4,128)} %multiply_select_fusion.scalars_ref.ends_ref, s32[4,64]{1,0:T(4,128)} %multiply_select_fusion.scalars_ref.ends_ref, f32[3,48,128]{2,1,0:T(8,128)} %bitcast.13, f32[3,48,128]{2,1,0:T(8,128)} %bitcast.14, s32[64,128,128]{2,1,0:T(8,128)} %bonds_hbm.1), custom_call_target="tpu_custom_call" | custom-call | tf_op jit(solution)/shard_map/pallas_call | solution.py:268
  25.7 1.6 %add_bitcast_fusion = f32[48,3,128]{2,0,1:T(8,128)} fusion(f32[3,48,128]{2,1,0:T(8,128)} %get-tuple-element.7, f32[3,48,128]{2,1,0:T(8,128)} %get-tuple-element.8), kind=kLoop, calls=%fused_computation | loop fusion | flops 18432 | bytes 221184 | tf_op jit(solution)/shard_map/transpose | solution.py:293
  (2 shorter events, 0.0 us)
